TPU v7x, 32 devices: a whole 2x2x4 slice. The times are simulated.
32 devices in a mesh: dp: 2 (over y), seq: 16 (over z, x, core).
Axes of the slice: x: 2, y: 2, z: 4, core: 2. Of those that a mesh axis runs over, the one named last changes fastest.
Arguments:
- features: bfloat16 [4096, 320], P(('dp', 'seq')), parts along dimension 0, may hold values from -40 to 40
- hint: bfloat16 [4096, 320], P(('dp', 'seq')), parts along dimension 0, may hold values from -6 to 6
- conv_weight: bfloat16 [3, 3, 320, 320], replicated, may hold values from -0.109375 to 0.109375
- conv_bias: float32 [320], replicated, may hold values from -3 to 3
- zero_weight: bfloat16 [320, 320], replicated, may hold values from -0.3125 to 0.3125
- zero_bias: float32 [320], replicated, may hold values from -2 to 2
- group_gain: float32 [320], replicated, may hold values from 0.5 to 1.5
- proj_in: bfloat16 [320, 320], replicated, may hold values from -0.3125 to 0.3125
- norm_gain: float32 [320], replicated, may hold values from 0.5 to 1.5
- query_weight: bfloat16 [320, 320], replicated, may hold values from -2 to 2
- key_weight: bfloat16 [320, 320], replicated, may hold values from -2 to 2
- value_weight: bfloat16 [320, 320], replicated, may hold values from -0.3125 to 0.3125
- attn_out: bfloat16 [320, 320], replicated, may hold values from -0.3125 to 0.3125
- proj_out: bfloat16 [320, 320], replicated, may hold values from -0.3125 to 0.3125
Outputs:
- block_out: bfloat16 [4096, 320], P(('dp', 'seq')), parts along dimension 0
There are 2 independent parts, one for each index of `dp`. A program takes and returns all parts, laid end to end along the dimension named above; an argument that names none is the same for every part. Nothing has to cross between parts.
All inputs are finite; a program needn't handle non-finite values.
Results may differ from a plain program's by a relative error of at most 0.023.
Values may be sent and summed in bfloat16 or wider, within the bound.
A program may use at most 64 MiB of HBM per device.

v0:
```python
import functools
import math

import jax
import jax.numpy as jnp
from jax import lax
from jax.experimental import pallas as pl
from jax.experimental.pallas import tpu as pltpu
from jax.sharding import PartitionSpec as P

HEADS = 8
GROUPS = 32
WIDTH = 128
CORES = 2

norm_eps = 1e-06
layer_eps = 1e-05
MESH = pl.DeviceIdType.MESH
F32 = jnp.float32
BF16 = jnp.bfloat16


def mm(x, y):
    return jnp.dot(x, y, preferred_element_type=F32)


def block_kernel(
    n, rows_a, rows_b,
    features, hint, conv_bias, zero_bias, group_gain, norm_gain,
    conv_hbm, zero_hbm, proj_in_hbm, query_hbm, key_hbm, value_hbm, attn_hbm, proj_hbm,
    out,
    conv_w, zero_w, proj_in_w, query_w, key_w, value_w, attn_w, proj_w,
    ext, gathered, keys_all, keys_t, qmask, scores, mixed,
    load_sem, halo_send, halo_recv, send_sem, recv_sem,
):
    channels, tokens = features.shape
    head_dim = channels // HEADS
    per_group = channels // GROUPS
    me = lax.axis_index("seq")
    core = lax.rem(me, CORES)
    chip = lax.div(me, CORES)
    b = lax.rem(chip, rows_b)
    a = lax.div(chip, rows_b)

    def device(aa, bb, cc):
        return (aa * rows_b + bb) * CORES + cc

    def as_columns(vector):
        return jnp.transpose(jnp.broadcast_to(vector[...].reshape(1, channels), (WIDTH, channels)))[:, :1]

    loads = {}
    for slot, (name, src, dst) in enumerate((
        ("conv", conv_hbm, conv_w), ("zero", zero_hbm, zero_w), ("proj_in", proj_in_hbm, proj_in_w),
        ("query", query_hbm, query_w), ("key", key_hbm, key_w), ("value", value_hbm, value_w),
        ("attn", attn_hbm, attn_w), ("proj", proj_hbm, proj_w),
    )):
        loads[name] = pltpu.make_async_copy(src, dst, load_sem.at[slot])
        loads[name].start()

    barrier = pltpu.get_barrier_semaphore()
    always = jnp.int32(1)
    peers = [
        (me > 0, me - 1), (me < n - 1, me + 1),
        (a > 0, device(a - 1, b, core)), (a < rows_a - 1, device(a + 1, b, core)),
        (None, device(a, b, 1 - core)),
    ]
    for k in range(1, rows_b):
        peers.append((None, device(a, lax.rem(b + k, rows_b), core)))
    count = jnp.int32(0)
    for cond, peer in peers:
        def greet(peer=peer):
            pl.semaphore_signal(barrier, inc=1, device_id={"seq": peer}, device_id_type=MESH)
        if cond is None:
            greet()
            count = count + always
        else:
            pl.when(cond)(greet)
            count = count + cond.astype(jnp.int32)
    pl.semaphore_wait(barrier, count)

    to_next = pltpu.make_async_remote_copy(
        hint.at[:, pl.ds(tokens - WIDTH, WIDTH)], ext.at[:, pl.ds(0, WIDTH)],
        halo_send.at[0], halo_recv.at[0], device_id={"seq": me + 1}, device_id_type=MESH)
    to_prev = pltpu.make_async_remote_copy(
        hint.at[:, pl.ds(0, WIDTH)], ext.at[:, pl.ds(WIDTH + tokens, WIDTH)],
        halo_send.at[1], halo_recv.at[1], device_id={"seq": me - 1}, device_id_type=MESH)
    pl.when(me < n - 1)(to_next.start)
    pl.when(me > 0)(to_prev.start)

    ext[:, pl.ds(WIDTH, tokens)] = hint[...]

    @pl.when(me == 0)
    def _():
        ext[:, pl.ds(0, WIDTH)] = jnp.zeros((channels, WIDTH), BF16)

    @pl.when(me == n - 1)
    def _():
        ext[:, pl.ds(WIDTH + tokens, WIDTH)] = jnp.zeros((channels, WIDTH), BF16)

    middle = jnp.transpose(hint[...])
    loads["conv"].wait()
    taps = [mm(middle, conv_w[1, d]) for d in range(3)]
    pl.when(me > 0)(to_next.wait_recv)
    pl.when(me < n - 1)(to_prev.wait_recv)
    for dy in (0, 2):
        lines = jnp.transpose(ext[:, pl.ds(dy * WIDTH, tokens)])
        taps = [taps[d] + mm(lines, conv_w[dy, d]) for d in range(3)]
    column = lax.rem(lax.broadcasted_iota(jnp.int32, (tokens, channels), 0), WIDTH)
    left = jnp.where(column == 0, 0.0, pltpu.roll(taps[0], 1, 0))
    right = jnp.where(column == WIDTH - 1, 0.0, pltpu.roll(taps[2], tokens - 1, 0))
    conv = left + taps[1] + right + conv_bias[...].reshape(1, channels)
    control = (conv / (1.0 + jnp.exp(-conv))).astype(BF16)
    loads["zero"].wait()
    branch = mm(control, zero_w[...]) + zero_bias[...].reshape(1, channels)
    merged = (features[...].astype(F32) + jnp.transpose(branch)).astype(BF16)
    gathered[me] = merged

    pending = []

    def send(src, target, cond):
        slot = len(pending)
        copy = pltpu.make_async_remote_copy(
            gathered.at[src], gathered.at[src], send_sem.at[slot], recv_sem.at[src],
            device_id={"seq": target}, device_id_type=MESH)
        pending.append((cond, copy))
        if cond is None:
            copy.start()
        else:
            pl.when(cond)(copy.start)

    def arrive(src, cond):
        def wait():
            pltpu.make_async_remote_copy(
                gathered.at[src], gathered.at[src], send_sem.at[0], recv_sem.at[src],
                device_id={"seq": me}, device_id_type=MESH).wait_recv()
        if cond is None:
            wait()
        else:
            pl.when(cond)(wait)

    def both(first, second):
        return second if first is None else first & second

    def to_partner(src, cond):
        send(src, device(a, b, 1 - core), cond)

    def along_b(src, cond):
        for k in range(1, rows_b):
            send(src, device(a, lax.rem(b + k, rows_b), core), cond)

    def from_b(aa, cond):
        for k in range(1, rows_b):
            src = device(aa, lax.rem(b + k, rows_b), core)
            arrive(src, cond)
            yield src

    even, odd = core == 0, core == 1
    up, down = a < rows_a - 1, a > 0

    along_b(me, None)
    send(me, device(a + 1, b, core), up)
    send(me, device(a - 1, b, core), down)
    to_partner(me, None)

    for name in ("proj_in", "query", "key", "value", "attn", "proj"):
        loads[name].wait()
    for weight in (proj_in_w, query_w, value_w, attn_w, proj_w):
        weight[...] = jnp.transpose(weight[...])
    gain, layer_gain = as_columns(group_gain), as_columns(norm_gain)
    row_group = lax.div(lax.broadcasted_iota(jnp.int32, (channels, channels), 0), jnp.int32(per_group))
    col_group = lax.div(lax.broadcasted_iota(jnp.int32, (channels, channels), 1), jnp.int32(per_group))
    same = (row_group == col_group).astype(F32)

    def group_sum(partial):
        total = jnp.dot(same, partial, preferred_element_type=F32, precision=lax.Precision.HIGHEST)
        return jnp.sum(total, axis=1, keepdims=True)

    shift = group_sum(merged.astype(F32)) / (tokens * per_group)

    for src in from_b(a, None):
        send(src, device(a + 1, b, core), even & up)
        send(src, device(a - 1, b, core), even & down)
        to_partner(src, None)
    for step in range(1, rows_a):
        for sign, more in ((-1, up), (1, down)):
            aa = a + sign * step
            inside = (aa >= 0) & (aa < rows_a)
            src = device(aa, b, core)
            arrive(src, inside)
            send(src, device(a - sign, b, core), inside & more)
            along_b(src, inside & odd)
            to_partner(src, inside)
            for k in range(1, rows_b):
                src = device(aa, lax.rem(b + k, rows_b), core)
                arrive(src, inside & even)
                send(src, device(a - sign, b, core), inside & more & even)
                to_partner(src, inside & even)
        for sign in (-1, 1):
            aa = a + sign * step
            inside = (aa >= 0) & (aa < rows_a) & odd
            for src in from_b(aa, inside):
                to_partner(src, inside)

    def add_block(src, acc):
        apart = gathered[src].astype(F32) - shift
        return acc[0] + apart, acc[1] + apart * apart

    zero_acc = jnp.zeros((channels, tokens), F32)
    sums = lax.fori_loop(0, n // CORES, lambda k, acc: add_block(k * CORES + core, acc), (zero_acc, zero_acc))
    for k in range(n // CORES):
        arrive(k * CORES + 1 - core, None)
        sums = add_block(k * CORES + 1 - core, sums)
    entry_count = tokens * n * per_group
    apart_mean = group_sum(sums[0]) / entry_count
    mean = shift + apart_mean
    var = jnp.maximum(group_sum(sums[1]) / entry_count - apart_mean * apart_mean, 0.0)
    inv = lax.rsqrt(var + norm_eps) * gain

    def project_norm(block):
        grouped = ((block.astype(F32) - mean) * inv).astype(BF16)
        inner = mm(proj_in_w[...], grouped).astype(BF16).astype(F32)
        centred = inner - jnp.mean(inner, axis=0, keepdims=True)
        spread = jnp.mean(jnp.square(centred), axis=0, keepdims=True)
        return inner, (centred * lax.rsqrt(spread + layer_eps) * layer_gain).astype(BF16)

    inner_own, normed_own = project_norm(merged)
    chunk = 4 if n % 4 == 0 else 1

    def norm_chunk(k, carry):
        block = jnp.concatenate([gathered[k * chunk + i] for i in range(chunk)], axis=1)
        normed = project_norm(block)[1]
        start = pl.multiple_of(k * chunk * tokens, chunk * tokens)
        keys_t[:, pl.ds(start, chunk * tokens)] = normed
        keys_all[pl.ds(start, chunk * tokens)] = jnp.transpose(normed)
        return carry

    lax.fori_loop(0, n // chunk, norm_chunk, 0)

    queries = mm(query_w[...], normed_own)
    row_head = lax.div(lax.broadcasted_iota(jnp.int32, (channels, tokens), 0), jnp.int32(head_dim))
    for h in range(HEADS):
        qmask[:, h * tokens:(h + 1) * tokens] = jnp.where(row_head == h, queries, 0.0).astype(BF16)
    scale = math.log2(math.e) / math.sqrt(head_dim)
    qmask[...] = (mm(key_w[...], qmask[...]) * scale).astype(BF16)

    pair = 2 * tokens
    def score(h2):
        scores[h2 % 2] = mm(keys_all[...], qmask[:, h2 * pair:(h2 + 1) * pair])

    score(0)
    for h2 in range(HEADS // 2):
        if h2 + 1 < HEADS // 2:
            score(h2 + 1)
        top = jnp.max(scores[h2 % 2], axis=0, keepdims=True)
        weights = jnp.exp2(scores[h2 % 2] - top)
        total = jnp.sum(weights, axis=0, keepdims=True)
        folded = (mm(keys_t[...], weights.astype(BF16)) / total).astype(BF16)
        values = mm(value_w[...], folded)
        for j in range(2):
            h = 2 * h2 + j
            mixed[pl.ds(h * head_dim, head_dim)] = values[h * head_dim:(h + 1) * head_dim, j * tokens:(j + 1) * tokens]
    after = (inner_own + mm(attn_w[...], mixed[...].astype(BF16))).astype(BF16)
    out[...] = (merged.astype(F32) + mm(proj_w[...], after)).astype(BF16)

    pl.when(me < n - 1)(to_next.wait_send)
    pl.when(me > 0)(to_prev.wait_send)
    for cond, copy in pending:
        if cond is None:
            copy.wait_send()
        else:
            pl.when(cond)(copy.wait_send)


def local(
    n, features, hint, conv_weight, conv_bias, zero_weight, zero_bias, group_gain, proj_in,
    norm_gain, query_weight, key_weight, value_weight, attn_out, proj_out,
):
    tokens, channels = features.shape
    chips = n // CORES
    rows_a = math.gcd(chips, 4)
    rows_b = chips // rows_a
    sends = 2 + rows_b + 3 * (rows_b - 1) + (rows_a - 1) * 2 * (1 + rows_b + 3 * (rows_b - 1))
    square = pltpu.VMEM((channels, channels), BF16)
    vmem = pl.BlockSpec(memory_space=pltpu.VMEM)
    hbm = pl.BlockSpec(memory_space=pl.ANY)
    result = pl.pallas_call(
        functools.partial(block_kernel, n, rows_a, rows_b),
        out_shape=jax.ShapeDtypeStruct((channels, tokens), BF16),
        in_specs=[vmem] * 6 + [hbm] * 8,
        out_specs=vmem,
        scratch_shapes=[
            pltpu.VMEM(conv_weight.shape, BF16), square, square, square, square, square, square, square,
            pltpu.VMEM((channels, tokens + 2 * WIDTH), BF16),
            pltpu.VMEM((n, channels, tokens), BF16),
            pltpu.VMEM((n * tokens, channels), BF16),
            pltpu.VMEM((channels, n * tokens), BF16),
            pltpu.VMEM((channels, HEADS * tokens), BF16),
            pltpu.VMEM((2, n * tokens, 2 * tokens), F32),
            pltpu.VMEM((channels, tokens), F32),
            pltpu.SemaphoreType.DMA((8,)),
            pltpu.SemaphoreType.DMA((2,)),
            pltpu.SemaphoreType.DMA((2,)),
            pltpu.SemaphoreType.DMA((sends,)),
            pltpu.SemaphoreType.DMA((n,)),
        ],
        compiler_params=pltpu.CompilerParams(
            collective_id=0, has_side_effects=True, vmem_limit_bytes=60 * 1024 * 1024),
    )(features.T, hint.T, conv_bias, zero_bias, group_gain, norm_gain,
      conv_weight, zero_weight, proj_in, query_weight, key_weight, value_weight, attn_out, proj_out)
    return result.T


def solution(mesh):
    split = P(("dp", "seq"), None)
    return jax.shard_map(
        functools.partial(local, mesh.shape["seq"]), mesh=mesh,
        in_specs=(split, split) + (P(),) * 12, out_specs=split, check_vma=False,
    )
```

profile of v0, /device:TPU:0, one launch (start us, length us, event | category | flops | bytes accessed | tf_op | source)
XLA Modules:
  0.0 38.6 jit_solution(15618462230706256747)
XLA Ops:
  0.0 37.1 %shard_map.136 = bf16[320,128]{1,0:T(8,128)(2,1)} custom-call(bf16[320,128]{1,0:T(8,128)(2,1)} %bitcast.4, bf16[320,128]{1,0:T(8,128)(2,1)} %bitcast.5, f32[320]{0:T(512)} %conv_bias.1, f32[320]{0:T(512)} %zero_bias.1, f32[320]{0:T(512)} %group_gain.1, f32[320]{0:T(512)} %norm_gain.1, bf16[3,3,320,320]{3,2,1,0:T(8,128)(2,1)} %conv_hbm.1, ...), custom_call_target="tpu_custom_call" | custom-call | tf_op jit(solution)/shard_map/pallas_call | solution.py:286
  37.1 1.5 %copy.16 = bf16[128,320]{0,1:T(8,128)(2,1)} copy(bf16[128,320]{0,1:T(8,128)(2,1)} %bitcast.3) | data formatting | bytes 163840
where the time goes:
time: 38.8 us; the launch traced here: 38.6 us
  Pallas kernels  37.1 us (96%)
  local copies, waits for them, and re-layouts  1.53 us (4%)
    pallas_call x1, Pallas kernels, local(): pl.pallas_call(functools.partial(block_kernel, n, rows_a, rows_b), out_sh...  37.1 us
    unnamed x1, local copies, waits for them, and re-layouts  1.53 us

commit v1 on v0

v1 whole, which is shorter than its diff:
```python
import functools
import math

import jax
import jax.numpy as jnp
from jax import lax
from jax.experimental import pallas as pl
from jax.experimental.pallas import tpu as pltpu
from jax.sharding import PartitionSpec as P

HEADS = 8
GROUPS = 32
WIDTH = 128
CORES = 2
LANES = 128
PIECES = 2
PLAN = (
    "r1", "s", "q", "x0", "k0", "r2", "o0", "w0", "x1", "k1", "r3", "p0o1", "x2", "k2",
    "w1", "p1o2", "x3", "k3", "w2", "p2o3", "w3", "p3",
)
EARLY = ()
SENDS = ("3","1","s")

norm_eps = 1e-06
layer_eps = 1e-05
MESH = pl.DeviceIdType.MESH
F32 = jnp.float32
BF16 = jnp.bfloat16
LOWEST = -3.0e38


def mm(x, y):
    return jnp.dot(x, y, preferred_element_type=F32)


def mm_t(x, y):
    return lax.dot_general(x, y, (((1,), (1,)), ((), ())), preferred_element_type=F32)


def split3(x):
    hi = x.astype(BF16)
    rest = x - hi.astype(F32)
    mid = rest.astype(BF16)
    lo = (rest - mid.astype(F32)).astype(BF16)
    return hi, mid, lo


def row_order(rows_a):
    return [sorted(range(rows_a), key=lambda aa: (abs(aa - a), abs(2 * aa - rows_a + 1))) for a in range(rows_a)]


def block_kernel(
    n, rows_a, rows_b,
    features_hbm, hint_hbm, conv_bias_hbm, zero_bias_hbm, group_gain_hbm, norm_gain_hbm,
    conv_hbm, zero_hbm, proj_in_hbm, query_hbm, key_hbm, value_hbm, attn_hbm, proj_hbm,
    out,
    features, hint, conv_bias, zero_bias, group_gain, norm_gain,
    conv_w, zero_w, proj_in_w, query_w, key_w, value_w, attn_w, proj_w,
    halo, gathered, kbuf, vbuf, qbd, stats, same, expand, zero_col, gain_col, layer_col, mean_bc, inv_bc,
    inner_own, top, total, acc,
    load_sem, halo_send, halo_recv, token, stat_send, stat_recv, send_sem, recv_sem, kv_send, kv_recv,
):
    channels, tokens = out.shape
    head_dim = channels // HEADS
    per_group = channels // GROUPS
    pairs = HEADS // 2
    pair_dim = 2 * head_dim
    me = lax.axis_index("seq")
    core = lax.rem(me, CORES)
    chip = lax.div(me, CORES)
    b = lax.rem(chip, rows_b)
    a = lax.div(chip, rows_b)

    def device(aa, bb, cc):
        return (aa * rows_b + bb) * CORES + cc

    loads = {}
    for slot, (name, src, dst) in enumerate((
        ("hint", hint_hbm, hint), ("conv", conv_hbm, conv_w), ("zero", zero_hbm, zero_w),
        ("features", features_hbm, features), ("conv_bias", conv_bias_hbm, conv_bias),
        ("zero_bias", zero_bias_hbm, zero_bias), ("group_gain", group_gain_hbm, group_gain),
        ("norm_gain", norm_gain_hbm, norm_gain), ("proj_in", proj_in_hbm, proj_in_w),
        ("query", query_hbm, query_w), ("key", key_hbm, key_w), ("value", value_hbm, value_w),
        ("attn", attn_hbm, attn_w), ("proj", proj_hbm, proj_w),
    )):
        loads[name] = pltpu.make_async_copy(src, dst, load_sem.at[slot])
        loads[name].start()

    pending = []

    def when(cond, fn):
        if cond is None:
            fn()
        else:
            pl.when(cond)(fn)

    def signal(sem, peer):
        pl.semaphore_signal(sem, inc=1, device_id={"seq": peer}, device_id_type=MESH)

    up, down = a < rows_a - 1, a > 0

    def as_int(cond):
        return cond.astype(jnp.int32)

    barrier = pltpu.get_barrier_semaphore()
    last_in_row = (b == rows_b - 1) & (core == 1) & up
    first_in_row = (b == 0) & (core == 0) & down
    mates = [(k, j) for k in range(rows_b) for j in range(CORES) if (k, j) != (0, 0)]
    for k, j in mates:
        signal(barrier, device(a, lax.rem(b + k, rows_b), lax.rem(core + j, CORES)))
    for cond, peer in ((up, device(a + 1, b, core)), (down, device(a - 1, b, core)),
                       (last_in_row, me + 1), (first_in_row, me - 1)):
        when(cond, functools.partial(signal, barrier, peer))
    pl.semaphore_wait(barrier, len(mates) + as_int(up) + as_int(down) + as_int(last_in_row) + as_int(first_in_row))

    loads["hint"].wait()
    to_next = pltpu.make_async_remote_copy(
        hint.at[:, pl.ds(tokens - WIDTH, WIDTH)], halo.at[0], halo_send.at[0], halo_recv.at[0], device_id={"seq": me + 1}, device_id_type=MESH)
    to_prev = pltpu.make_async_remote_copy(
        hint.at[:, pl.ds(0, WIDTH)], halo.at[1], halo_send.at[1], halo_recv.at[1], device_id={"seq": me - 1}, device_id_type=MESH)
    pl.when(me < n - 1)(to_next.start)
    pl.when(me > 0)(to_prev.start)

    when(up, functools.partial(signal, token.at[0], device(a + 1, b, core)))
    when(down, functools.partial(signal, token.at[0], device(a - 1, b, core)))

    @pl.when(me == 0)
    def _():
        halo[0] = jnp.zeros((channels, WIDTH), BF16)

    @pl.when(me == n - 1)
    def _():
        halo[1] = jnp.zeros((channels, WIDTH), BF16)

    row_group = lax.div(lax.broadcasted_iota(jnp.int32, (channels, channels), 0), jnp.int32(per_group))
    col_group = lax.div(lax.broadcasted_iota(jnp.int32, (channels, channels), 1), jnp.int32(per_group))
    same[...] = (row_group == col_group).astype(BF16)
    expand[...] = (
        lax.div(lax.broadcasted_iota(jnp.int32, (channels, LANES), 0), jnp.int32(per_group))
        == lax.broadcasted_iota(jnp.int32, (channels, LANES), 1)).astype(BF16)

    def as_columns(vector):
        return jnp.transpose(jnp.broadcast_to(vector[...].reshape(1, channels), (LANES, channels)))

    loads["conv"].wait()
    middle = jnp.transpose(hint[...])
    taps = [mm(middle, conv_w[1, d]) for d in range(3)]
    for name in ("zero", "features", "conv_bias", "zero_bias", "group_gain", "norm_gain"):
        loads[name].wait()
    zero_w[...] = jnp.transpose(zero_w[...])
    zero_col[...] = as_columns(zero_bias)
    gain_col[...] = as_columns(group_gain)
    layer_col[...] = as_columns(norm_gain)
    for name in ("proj_in", "query", "key", "value", "attn", "proj"):
        loads[name].wait()
    for weight in (proj_in_w, query_w, key_w, value_w, attn_w, proj_w):
        weight[...] = jnp.transpose(weight[...])

    pl.semaphore_wait(token.at[0], as_int(up) + as_int(down))
    up2, down2 = a + 2 < rows_a, a >= 2
    when(up2, functools.partial(signal, token.at[1], device(a + 2, b, core)))
    when(down2, functools.partial(signal, token.at[1], device(a - 2, b, core)))

    pl.when(me > 0)(to_next.wait_recv)
    pl.when(me < n - 1)(to_prev.wait_recv)
    for k, dy in enumerate((0, 2)):
        line = jnp.transpose(halo[k])
        if tokens > WIDTH:
            line = jnp.concatenate([line, middle[:-WIDTH]] if k == 0 else [middle[WIDTH:], line], axis=0)
        taps = [taps[d] + mm(line, conv_w[dy, d]) for d in range(3)]
    column = lax.rem(lax.broadcasted_iota(jnp.int32, (tokens, channels), 0), WIDTH)
    left = jnp.where(column == 0, 0.0, pltpu.roll(taps[0], 1, 0))
    right = jnp.where(column == WIDTH - 1, 0.0, pltpu.roll(taps[2], tokens - 1, 0))
    conv = left + taps[1] + right + conv_bias[...].reshape(1, channels)
    control = (conv / (1.0 + jnp.exp(-conv))).astype(BF16)
    branch = mm_t(zero_w[...], control) + zero_col[...]
    merged = (features[...].astype(F32) + branch).astype(BF16)
    gathered[a, b] = merged

    part = channels // PIECES

    def piece(aa, bb, h):
        return gathered.at[aa, bb, pl.ds(h * part, part)]

    def send(aa, bb, h, target, cond):
        slot = len(pending)
        copy = pltpu.make_async_remote_copy(
            piece(aa, bb, h), piece(aa, bb, h), send_sem.at[slot], recv_sem.at[aa, bb, h],
            device_id={"seq": target}, device_id_type=MESH)
        pending.append((cond, copy))
        when(cond, copy.start)

    def arrive(aa, bb, h):
        pltpu.make_async_remote_copy(
            piece(aa, bb, h), piece(aa, bb, h), send_sem.at[0], recv_sem.at[aa, bb, h],
            device_id={"seq": me}, device_id_type=MESH).wait_recv()

    def across(aa, h, cond):
        for k in range(1, rows_b):
            send(aa, b, h, device(a, lax.rem(b + k, rows_b), core), cond)

    def relay(step):
        for h in range(PIECES):
            for sign, inside, more in ((1, a + step < rows_a, down), (-1, a >= step, up)):
                aa = a + sign * step
                pl.when(inside)(functools.partial(arrive, aa, b, h))
                if step + 1 < rows_a and str(step + 1) not in EARLY + SENDS:
                    send(aa, b, h, device(a - sign, b, core), inside & more)
                if str(step) + "x" not in EARLY + SENDS:
                    across(aa, h, inside)

    def direct(step, columns):
        for h in range(PIECES):
            for sign, inside in ((-1, a >= step), (1, a + step < rows_a)):
                for k in columns:
                    send(a, b, h, device(a + sign * step, lax.rem(b + k, rows_b), core), inside)

    def launch(words):
        for word in words:
            if word == "s":
                for h in range(PIECES):
                    across(a, h, None)
            else:
                direct(int(word[0]), range(1, rows_b) if word[1:] else range(1))

    launch(EARLY)

    by_token = jnp.transpose(merged).astype(F32)
    shift = by_token[:1]
    apart = by_token - shift
    first = jnp.sum(apart, axis=0, keepdims=True)
    second = jnp.sum(apart * apart, axis=0, keepdims=True)
    channel_mean = shift + first * (1.0 / tokens)
    channel_dev = jnp.maximum(second - first * first * (1.0 / tokens), 0.0)

    def stack_rows(rows):
        fill = 16 - len(rows)
        return jnp.concatenate(rows + [jnp.zeros((fill,) + rows[0].shape[1:], BF16)], axis=0)

    spread = mm(stack_rows(list(split3(channel_mean))), same[...])
    group_mean = jnp.sum(spread[:3], axis=0, keepdims=True) * (1.0 / per_group)
    off = channel_mean - group_mean
    group_dev = channel_dev + tokens * off * off
    packed = mm(stack_rows(list(split3(channel_mean)) + list(split3(group_dev))), expand[...])
    stats[me] = jnp.concatenate([
        jnp.sum(packed[:3], axis=0, keepdims=True) * (1.0 / per_group),
        jnp.sum(packed[3:6], axis=0, keepdims=True)], axis=0)

    pl.semaphore_wait(token.at[1], as_int(up2) + as_int(down2))
    stat_copies = []
    for k in range(1, n):
        copy = pltpu.make_async_remote_copy(
            stats.at[me], stats.at[me], stat_send.at[k], stat_recv.at[me],
            device_id={"seq": lax.rem(me + k, n)}, device_id_type=MESH)
        copy.start()
        stat_copies.append(copy)

    launch(SENDS)

    def stat_wait(src):
        pltpu.make_async_remote_copy(
            stats.at[src], stats.at[src], stat_send.at[0], stat_recv.at[src],
            device_id={"seq": me}, device_id_type=MESH).wait_recv()

    def combine():
        for k in range(1, n):
            stat_wait(lax.rem(me + k, n))
        count = tokens * per_group
        every = [stats[k] for k in range(n)]
        mean = functools.reduce(jnp.add, [s[:1] for s in every]) * (1.0 / n)
        dev = functools.reduce(jnp.add, [s[1:2] + count * jnp.square(s[:1] - mean) for s in every])
        inv = lax.rsqrt(dev * (1.0 / (count * n)) + norm_eps)

        def stand(row):
            return jnp.transpose(jnp.broadcast_to(row, (LANES, LANES)))

        standing = split3(jnp.concatenate([stand(mean), stand(inv)], axis=1))
        columns = functools.reduce(jnp.add, [mm(expand[...], part3) for part3 in standing])
        mean_bc[...] = columns[:, :LANES]
        inv_bc[...] = columns[:, LANES:] * gain_col[...]

    def wide(block, width):
        return jnp.concatenate([block] * (width // LANES), axis=1)

    def project_norm(blocks):
        width = tokens * len(blocks)
        scaled = jnp.concatenate([
            ((block.astype(F32) - wide(mean_bc[...], tokens)) * wide(inv_bc[...], tokens)).astype(BF16)
            for block in blocks], axis=1)
        inner = mm(proj_in_w[...], scaled)
        centred = inner - jnp.mean(inner, axis=0, keepdims=True)
        spread = jnp.mean(jnp.square(centred), axis=0, keepdims=True)
        return inner, (centred * lax.rsqrt(spread + layer_eps) * wide(layer_col[...], width)).astype(BF16)

    in_first = lax.broadcasted_iota(jnp.int32, (pair_dim, tokens), 0) < head_dim

    def own_queries():
        inner, normed = project_norm([gathered[a, b]])
        inner_own[...] = inner
        scale = math.log2(math.e) / math.sqrt(head_dim)
        queries = mm(query_w[...], normed) * scale
        for p in range(pairs):
            rows = queries[p * pair_dim:(p + 1) * pair_dim]
            qbd[p] = jnp.concatenate(
                [jnp.where(in_first, rows, 0.0), jnp.where(in_first, 0.0, rows)], axis=1).astype(BF16)
        top[...] = jnp.full(top.shape, LOWEST, F32)
        total[...] = jnp.zeros(total.shape, F32)
        acc[...] = jnp.zeros(acc.shape, F32)

    group = 2 if rows_b % 2 == 0 else 1
    chunk = group * tokens
    kv_copies = []

    def beside(aa):
        for h in range(PIECES):
            for k in range(1, rows_b):
                arrive(aa, lax.rem(b + k, rows_b), h)

    def make_kv(aa):
        for i in range(rows_b // group):
            normed = project_norm([gathered[aa, i * group + j] for j in range(group)])[1]
            keys = mm(key_w[...], normed).astype(BF16)
            vbuf[aa, core, :, i * chunk:(i + 1) * chunk] = mm(value_w[...], normed).astype(BF16)
            for p in range(pairs):
                kbuf[aa, core, p, i * chunk:(i + 1) * chunk] = jnp.transpose(keys[p * pair_dim:(p + 1) * pair_dim])
        for slot, buf in enumerate((kbuf, vbuf)):
            copy = pltpu.make_async_remote_copy(
                buf.at[aa, core], buf.at[aa, core], kv_send.at[aa, slot], kv_recv.at[aa, slot],
                device_id={"seq": device(a, b, 1 - core)}, device_id_type=MESH)
            copy.start()
            kv_copies.append(copy)

    def partner_kv(aa):
        for slot, buf in enumerate((kbuf, vbuf)):
            pltpu.make_async_remote_copy(
                buf.at[aa, 1 - core], buf.at[aa, 1 - core], kv_send.at[aa, slot], kv_recv.at[aa, slot],
                device_id={"seq": device(a, b, 1 - core)}, device_id_type=MESH).wait_recv()

    def attend(parts):
        for i in range(rows_b // group):
            span = slice(i * chunk, (i + 1) * chunk)
            scores = [[mm(kbuf[aa, side, p, span], qbd[p]) for aa, side in parts] for p in range(pairs)]
            for p in range(pairs):
                before = top[p]
                peaks = [jnp.max(s, axis=0, keepdims=True) for s in scores[p]]
                now = functools.reduce(jnp.maximum, peaks, before)
                weights = [jnp.exp2(s - now) for s in scores[p]]
                fade = jnp.exp2(before - now)
                total[p] = total[p] * fade + functools.reduce(
                    jnp.add, [jnp.sum(w, axis=0, keepdims=True) for w in weights])
                top[p] = now
                mixes = [mm(vbuf[aa, side, p * pair_dim:(p + 1) * pair_dim, span], w.astype(BF16))
                         for (aa, side), w in zip(parts, weights)]
                acc[p] = acc[p] * fade + functools.reduce(jnp.add, mixes)

    table = row_order(rows_a)
    order = [sum(table[a0][k] * as_int(a == a0) for a0 in range(rows_a)) for k in range(rows_a)]
    def plan(words):
        for word in words:
            kind, arg = word[0], word[1:]
            if kind == "r":
                if int(arg) < rows_a:
                    relay(int(arg))
            elif kind == "s":
                combine()
            elif kind == "q":
                own_queries()
            elif int(arg[0]) >= rows_a:
                pass
            elif kind == "x":
                beside(order[int(arg)])
            elif kind == "k":
                make_kv(order[int(arg)])
            elif kind == "w":
                partner_kv(order[int(arg)])
            else:
                attend([(order[int(t[1])], core if t[0] == "o" else 1 - core)
                        for t in (word[j:j + 2] for j in range(0, len(word), 2)) if int(t[1]) < rows_a])

    plan(PLAN)

    mixed = []
    for p in range(pairs):
        ratio = acc[p] / total[p]
        mixed.append(jnp.where(in_first, ratio[:, :tokens], ratio[:, tokens:]))
    mixed = jnp.concatenate(mixed, axis=0).astype(BF16)
    after = (inner_own[...] + mm(attn_w[...], mixed)).astype(BF16)
    out[...] = (gathered[a, b].astype(F32) + mm(proj_w[...], after)).astype(BF16)

    pl.when(me < n - 1)(to_next.wait_send)
    pl.when(me > 0)(to_prev.wait_send)
    for copy in stat_copies + kv_copies:
        copy.wait_send()
    for cond, copy in pending:
        when(cond, copy.wait_send)


def local(
    n, features, hint, conv_weight, conv_bias, zero_weight, zero_bias, group_gain, proj_in,
    norm_gain, query_weight, key_weight, value_weight, attn_out, proj_out,
):
    tokens, channels = features.shape
    chips = n // CORES
    rows_a = math.gcd(chips, 4)
    rows_b = chips // rows_a
    pairs = HEADS // 2
    pair_dim = channels // pairs
    sends = PIECES * (8 * rows_b + 2 * (rows_a - 1) * rows_b)
    square = pltpu.VMEM((channels, channels), BF16)
    vector = pltpu.VMEM((channels,), F32)
    block = pltpu.VMEM((channels, tokens), BF16)
    column = pltpu.VMEM((channels, LANES), F32)
    hbm = pl.BlockSpec(memory_space=pltpu.HBM)
    result = pl.pallas_call(
        functools.partial(block_kernel, n, rows_a, rows_b),
        out_shape=jax.ShapeDtypeStruct((channels, tokens), BF16),
        in_specs=[hbm] * 14,
        out_specs=pl.BlockSpec(memory_space=pltpu.VMEM),
        scratch_shapes=[
            block, block, vector, vector, vector, vector,
            pltpu.VMEM(conv_weight.shape, BF16), square, square, square, square, square, square, square,
            pltpu.VMEM((2, channels, WIDTH), BF16),
            pltpu.VMEM((rows_a, rows_b, channels, tokens), BF16),
            pltpu.VMEM((rows_a, CORES, pairs, rows_b * tokens, pair_dim), BF16),
            pltpu.VMEM((rows_a, CORES, channels, rows_b * tokens), BF16),
            pltpu.VMEM((pairs, pair_dim, 2 * tokens), BF16),
            pltpu.VMEM((n, 2, LANES), F32),
            square,
            pltpu.VMEM((channels, LANES), BF16),
            column, column, column, column, column,
            pltpu.VMEM((channels, tokens), F32),
            pltpu.VMEM((pairs, 1, 2 * tokens), F32),
            pltpu.VMEM((pairs, 1, 2 * tokens), F32),
            pltpu.VMEM((pairs, pair_dim, 2 * tokens), F32),
            pltpu.SemaphoreType.DMA((14,)),
            pltpu.SemaphoreType.DMA((2,)),
            pltpu.SemaphoreType.DMA((2,)),
            pltpu.SemaphoreType.REGULAR((2,)),
            pltpu.SemaphoreType.DMA((n,)),
            pltpu.SemaphoreType.DMA((n,)),
            pltpu.SemaphoreType.DMA((sends,)),
            pltpu.SemaphoreType.DMA((rows_a, rows_b, PIECES)),
            pltpu.SemaphoreType.DMA((rows_a, 2)),
            pltpu.SemaphoreType.DMA((rows_a, 2)),
        ],
        compiler_params=pltpu.CompilerParams(
            collective_id=0, has_side_effects=True, vmem_limit_bytes=40 * 1024 * 1024),
    )(*(pltpu.with_memory_space_constraint(x, pltpu.HBM) for x in (
        features.T, hint.T, conv_bias, zero_bias, group_gain, norm_gain,
        conv_weight, zero_weight, proj_in, query_weight, key_weight, value_weight, attn_out, proj_out)))
    return result.T


def solution(mesh):
    split = P(("dp", "seq"), None)
    return jax.shard_map(
        functools.partial(local, mesh.shape["seq"]), mesh=mesh,
        in_specs=(split, split) + (P(),) * 12, out_specs=split, check_vma=False,
    )
```

time: 38.8 us -> 27.4 us (0.71)
  Pallas kernels: 37.1 us -> 26.6 us
  local copies, waits for them, and re-layouts: 1.53 us -> 0.64 us
    pallas_call x1, Pallas kernels: 37.1 us -> 26.6 us  [local(): pl.pallas_call(functools.partial(block_kernel, n, rows_a, rows_b), out_sh...]
    unnamed x1, local copies, waits for them, and re-layouts: 1.53 us -> 0.64 us
where the time goes in v1:
time: 27.4 us; the launch traced here: 27.3 us
  Pallas kernels  26.6 us (97%)
  local copies, waits for them, and re-layouts  0.64 us (2%)
    pallas_call x1, Pallas kernels, local(): pl.pallas_call(functools.partial(block_kernel, n, rows_a, rows_b), out_sh...  26.6 us
    unnamed x1, local copies, waits for them, and re-layouts  0.64 us

profile of v1, /device:TPU:0, one launch (start us, length us, event | category | flops | bytes accessed | tf_op | source)
XLA Modules:
  0.0 27.3 jit_solution(16555974726167170402)
XLA Ops:
  0.0 26.6 %shard_map.136 = bf16[320,128]{1,0:T(8,128)(2,1)S(1)} custom-call(bf16[320,128]{1,0:T(8,128)(2,1)} %bitcast.4, bf16[320,128]{1,0:T(8,128)(2,1)} %bitcast.5, f32[320]{0:T(512)} %conv_bias_hbm.1, f32[320]{0:T(512)} %zero_bias_hbm.1, f32[320]{0:T(512)} %group_gain_hbm.1, f32[320]{0:T(512)} %norm_gain_hbm.1, bf16[3,3,320,320]{3,2,1,0:T(8,128)(2,1)} %conv_hbm.1, ...), custom_call_target="tpu_custom_call" | custom-call | tf_op jit(solution)/shard_map/pallas_call | solution.py:414
  26.6 0.6 %copy.16 = bf16[128,320]{0,1:T(8,128)(2,1)} copy(bf16[128,320]{0,1:T(8,128)(2,1)S(1)} %bitcast.3) | data formatting | bytes 163840

commit v2 on v1

--- a/solution.py
+++ b/solution.py
@@ -15,7 +15,7 @@
 LANES = 128
 PIECES = 2
 PLAN = (
-    "r1", "s", "q", "x0", "k0", "r2", "o0", "w0", "x1", "k1", "r3", "p0o1", "x2", "k2",
+    "r1", "s", "q", "x0", "k0", "r2", "r3", "o0", "w0", "x1", "k1", "p0o1", "x2", "k2",
     "w1", "p1o2", "x3", "k3", "w2", "p2o3", "w3", "p3",
 )
 EARLY = ()
@@ -161,13 +161,22 @@
     when(up2, functools.partial(signal, token.at[1], device(a + 2, b, core)))
     when(down2, functools.partial(signal, token.at[1], device(a - 2, b, core)))
 
-    pl.when(me > 0)(to_next.wait_recv)
-    pl.when(me < n - 1)(to_prev.wait_recv)
-    for k, dy in enumerate((0, 2)):
-        line = jnp.transpose(halo[k])
+    def line(k):
+        rows = jnp.transpose(halo[k])
         if tokens > WIDTH:
-            line = jnp.concatenate([line, middle[:-WIDTH]] if k == 0 else [middle[WIDTH:], line], axis=0)
-        taps = [taps[d] + mm(line, conv_w[dy, d]) for d in range(3)]
+            rows = jnp.where(
+                k == 0, jnp.concatenate([rows, middle[:-WIDTH]], axis=0),
+                jnp.concatenate([middle[WIDTH:], rows], axis=0))
+        return rows
+
+    pl.when(core == 0)(to_prev.wait_recv)
+    pl.when(core == 1)(to_next.wait_recv)
+    rows = line(1 - core)
+    taps = [taps[d] + mm(rows, conv_w[2 - 2 * core, d]) for d in range(3)]
+    pl.when((core == 0) & (me > 0))(to_next.wait_recv)
+    pl.when((core == 1) & (me < n - 1))(to_prev.wait_recv)
+    rows = line(core)
+    taps = [taps[d] + mm(rows, conv_w[2 * core, d]) for d in range(3)]
     column = lax.rem(lax.broadcasted_iota(jnp.int32, (tokens, channels), 0), WIDTH)
     left = jnp.where(column == 0, 0.0, pltpu.roll(taps[0], 1, 0))
     right = jnp.where(column == WIDTH - 1, 0.0, pltpu.roll(taps[2], tokens - 1, 0))

time: 27.4 us -> 27 us (0.985)
  Pallas kernels: 26.6 us -> 26.2 us
    pallas_call x1, Pallas kernels: 26.6 us -> 26.2 us  [local(): pl.pallas_call(functools.partial(block_kernel, n, rows_a, rows_b), out_sh...]
where the time goes in v2:
time: 27 us; the launch traced here: 26.8 us
  Pallas kernels  26.2 us (97%)
  local copies, waits for them, and re-layouts  0.64 us (2%)
    pallas_call x1, Pallas kernels, local(): pl.pallas_call(functools.partial(block_kernel, n, rows_a, rows_b), out_sh...  26.2 us
    unnamed x1, local copies, waits for them, and re-layouts  0.64 us

profile of v2, /device:TPU:0, one launch (start us, length us, event | category | flops | bytes accessed | tf_op | source)
XLA Modules:
  0.0 26.8 jit_solution(14745430773586272446)
XLA Ops:
  0.0 26.2 %shard_map.136 = bf16[320,128]{1,0:T(8,128)(2,1)S(1)} custom-call(bf16[320,128]{1,0:T(8,128)(2,1)} %bitcast.4, bf16[320,128]{1,0:T(8,128)(2,1)} %bitcast.5, f32[320]{0:T(512)} %conv_bias_hbm.1, f32[320]{0:T(512)} %zero_bias_hbm.1, f32[320]{0:T(512)} %group_gain_hbm.1, f32[320]{0:T(512)} %norm_gain_hbm.1, bf16[3,3,320,320]{3,2,1,0:T(8,128)(2,1)} %conv_hbm.1, ...), custom_call_target="tpu_custom_call" | custom-call | tf_op jit(solution)/shard_map/pallas_call | solution.py:423
  26.2 0.6 %copy.16 = bf16[128,320]{0,1:T(8,128)(2,1)} copy(bf16[128,320]{0,1:T(8,128)(2,1)S(1)} %bitcast.3) | data formatting | bytes 163840
